TPU v7x, 32 devices: a whole 2x2x4 slice. The times are simulated.
32 devices in a mesh: mem: 4 (over y, core), lat: 4 (over z), lon: 2 (over x).
Axes of the slice: x: 2, y: 2, z: 4, core: 2. Of those that a mesh axis runs over, the one named last changes fastest.
Arguments:
- fields: bfloat16 [4, 2, 96, 96, 512], P('mem', None, 'lat', 'lon'), may hold values from -6 to 6
- region: int32 [96, 96], P('lat', 'lon'), may hold values from 0 to 2
- gain_attn: float32 [512], replicated, may hold values from 0.1 to 1.9
- w_qkv: bfloat16 [512, 1536], P(None, ('mem', 'lat', 'lon')), may hold values from -1 to 1
- w_proj: bfloat16 [512, 512], P(None, ('mem', 'lat', 'lon')), may hold values from -0.25 to 0.25
- gain_mlp: float32 [512], replicated, may hold values from 0.1 to 1.9
- w_up: bfloat16 [512, 2048], P(None, ('mem', 'lat', 'lon')), may hold values from -0.25 to 0.25
- w_down: bfloat16 [2048, 512], P(None, ('mem', 'lat', 'lon')), may hold values from -0.125 to 0.125
Outputs:
- updated: bfloat16 [4, 2, 96, 96, 512], P('mem', None, 'lat', 'lon')
All inputs are finite; a program needn't handle non-finite values.
Results may differ from a plain program's by a relative error of at most 0.011.
Values may be sent and summed in bfloat16 or wider, within the bound.
A program may use at most 192 MiB of HBM per device.

v0:
```python
import jax
import jax.numpy as jnp
from jax import lax
from jax.sharding import PartitionSpec as P

HEADS = 16
HDIM = 32
WLAT = 6
WLON = 12
SH = 3
SL = 6


eps = 1e-05


def shifted_2(block, axis, distance):
    devices = range(lax.axis_size(axis))
    route = [((i - distance) % len(devices), i) for i in devices]
    return lax.ppermute(block, axis, route)


def layer_norm(values, gain_vec):
    values = values.astype(jnp.float32)
    average = jnp.mean(values, axis=-1, keepdims=True)
    centred = values - average
    variance = jnp.mean(centred * centred, axis=-1, keepdims=True)
    return (centred * lax.rsqrt(variance + eps) * gain_vec).astype(jnp.bfloat16)


def attend(qkv_all, region_ids, north_side, height):
    levels, row_count, col_count, width3 = qkv_all.shape
    width = width3 // 3
    band_count = row_count // height
    win_count = col_count // WLON
    win_tok = levels * height * WLON
    windowed = qkv_all.reshape(levels, band_count, height, win_count, WLON, width3)
    windowed = windowed.transpose(1, 3, 0, 2, 4, 5).reshape(
        band_count * win_count, win_tok, 3, HEADS, width // HEADS
    )
    ids_full = jnp.broadcast_to(region_ids[None], (levels, row_count, col_count))
    ids_full = ids_full.reshape(levels, band_count, height, win_count, WLON).transpose(
        1, 3, 0, 2, 4
    )
    ids_full = ids_full.reshape(band_count * win_count, win_tok)
    north_full = jnp.broadcast_to(north_side[None, :, None], (levels, row_count, col_count))
    north_full = north_full.reshape(levels, band_count, height, win_count, WLON).transpose(
        1, 3, 0, 2, 4
    )
    north_full = north_full.reshape(band_count * win_count, win_tok)
    scores = jnp.einsum(
        "wqhd,wkhd->whqk", windowed[:, :, 0], windowed[:, :, 1], preferred_element_type=jnp.float32
    )
    scores = scores * (1.0 / HDIM**0.5)
    allow = (ids_full[:, :, None] == ids_full[:, None, :]) & (
        north_full[:, :, None] == north_full[:, None, :]
    )
    scores = jnp.where(allow[:, None], scores, -1000000000.0)
    attn_probs = jax.nn.softmax(scores, axis=-1).astype(jnp.bfloat16)
    mixed_heads = jnp.einsum(
        "whqk,wkhd->wqhd", attn_probs, windowed[:, :, 2], preferred_element_type=jnp.float32
    )
    mixed_heads = mixed_heads.astype(jnp.bfloat16).reshape(
        band_count, win_count, levels, height, WLON, width
    )
    return mixed_heads.transpose(2, 0, 3, 1, 4, 5).reshape(levels, row_count, col_count, width)


def body(fields, region, gain_attn, w_qkv, w_proj, gain_mlp, w_up, w_down):
    member = fields[0]
    levels, clat, clon, width = member.shape
    normed = layer_norm(member, gain_attn)
    region_ids = region.astype(jnp.bfloat16)
    lat_pos = lax.axis_index("lat")
    nlat_all = clat * lax.axis_size("lat")
    row_ids = jnp.arange(clat, dtype=jnp.int32)
    north_side = (lat_pos * clat + SH + row_ids) % nlat_all < SH
    arrived, arrived_ids = shifted_2((normed[:, :SH], region_ids[:SH]), "lat", -1)
    lat_band = jnp.concatenate([normed[:, SH:], arrived], axis=1)
    band_ids = jnp.concatenate([region_ids[SH:], arrived_ids], axis=0)
    strip, strip_ids = shifted_2((lat_band[:, :, :SL], band_ids[:, :SL]), "lon", -1)
    shifted = jnp.concatenate([lat_band[:, :, SL:], strip], axis=2)
    shifted_ids = jnp.concatenate([band_ids[:, SL:], strip_ids], axis=1)
    tok_rows = shifted.reshape(-1, width)
    qkv_all = (
        jnp.dot(
            tok_rows,
            lax.all_gather(w_qkv, ("mem", "lat", "lon"), axis=1, tiled=True),
            preferred_element_type=jnp.float32,
        )
        .astype(jnp.bfloat16)
        .reshape(levels, clat, clon, 3 * width)
    )
    mixed_heads = attend(qkv_all, shifted_ids, north_side, WLAT)
    proj_tok_rows = mixed_heads.reshape(-1, width)
    attn_out = (
        jnp.dot(
            proj_tok_rows,
            lax.all_gather(w_proj, ("mem", "lat", "lon"), axis=1, tiled=True),
            preferred_element_type=jnp.float32,
        )
        .astype(jnp.bfloat16)
        .reshape(levels, clat, clon, width)
    )
    arrived_cols = shifted_2(attn_out[:, :, clon - SL :], "lon", 1)
    attn_out = jnp.concatenate([arrived_cols, attn_out[:, :, : clon - SL]], axis=2)
    arrived_rows = shifted_2(attn_out[:, clat - SH :], "lat", 1)
    attn_out = jnp.concatenate([arrived_rows, attn_out[:, : clat - SH]], axis=1)
    resid = (member.astype(jnp.float32) + attn_out.astype(jnp.float32)).astype(jnp.bfloat16)
    normed2 = layer_norm(resid, gain_mlp).reshape(-1, width)
    pre_act = jnp.dot(
        normed2,
        lax.all_gather(w_up, ("mem", "lat", "lon"), axis=1, tiled=True),
        preferred_element_type=jnp.float32,
    )
    hidden = jax.nn.gelu(pre_act, approximate=False).astype(jnp.bfloat16)
    delta = jnp.dot(
        hidden,
        lax.all_gather(w_down, ("mem", "lat", "lon"), axis=1, tiled=True),
        preferred_element_type=jnp.float32,
    ).reshape(levels, clat, clon, width)
    updated = (resid.astype(jnp.float32) + delta).astype(jnp.bfloat16)
    return updated[None]


def solution(mesh):
    in_specs = (
        P("mem", None, "lat", "lon", None),
        P("lat", "lon"),
        P(),
        P(None, ("mem", "lat", "lon")),
        P(None, ("mem", "lat", "lon")),
        P(),
        P(None, ("mem", "lat", "lon")),
        P(None, ("mem", "lat", "lon")),
    )
    out_specs = P("mem", None, "lat", "lon", None)
    return jax.shard_map(body, mesh=mesh, in_specs=in_specs, out_specs=out_specs, check_vma=False)
```

profile of v0, /device:TPU:0, one launch (start us, length us, event | category | flops | bytes accessed | tf_op | source)
XLA Modules:
  0.0 395.8 jit_solution(3137256965465653519)
XLA Ops:
  6.5 0.7 all-gather.4.cloned.1.call-update
  7.3 0.0 all-gather.6.cloned.1.call-start
  7.3 2.0 convert_reduce_fusion.1
  9.4 2.7 fusion.27
  12.1 0.9 fusion.29
  13.1 0.0 copy-start.5
  13.1 1.4 copy-done.5
  14.5 5.1 %collective-permute-start = (bf16[2,3,48,512]{3,2,1,0:T(8,128)(2,1)S(1)}, bf16[2,3,48,512]{3,2,1,0:T(8,128)(2,1)S(1)}, u32[]{:S(2)}, u32[]{:S(2)}) collective-permute-start(bf16[2,3,48,512]{3,2,1,0:T(8,128)(2,1)S(1)} %slice.61), channel_id=1, source_target_pairs={{2,0},{4,2},{6,4},{0,6},{3,1},{5,3},{7,5},{1,7},{10,8},{12,10},{14... | collective-permute-start | bytes 884744 | tf_op jit(solution)/shard_map/ppermute | solution.py:20
  19.7 0.5 collective-permute-start.2
  20.2 0.0 all-gather.6.cloned.1.call-update
  20.2 0.0 all-gather.8.cloned.1.call-start
  20.2 76.2 %all_gather.13 = bf16[512,512]{0,1:T(8,128)(2,1)} all-gather(bf16[512,16]{0,1:T(8,128)(2,1)S(1)} %copy-done.6), channel_id=1, replica_groups=mesh['mem'=4,'lat'=4,'lon'=2] {'mem','lat','lon'}, dimensions={1}, use_global_device_ids=true | all-gather | bytes 540672 | tf_op jit(solution)/shard_map/all_gather | solution.py:99
  96.5 1.8 slice.60
  98.3 0.1 transpose.33
  98.4 0.1 eq.44
  98.5 0.0 collective-permute-done.2
  98.5 0.1 collective-permute-start.3
  98.6 0.1 slice_maximum_fusion.1
  98.7 3.7 collective-permute-done.3
  102.4 0.1 pad_maximum_fusion.5
  102.5 0.1 broadcast_in_dim.12
  102.6 0.1 eq.40
  102.7 0.0 collective-permute-done
  102.8 0.1 collective-permute-start.1
  102.8 1.4 compare_and_fusion
  104.2 0.6 slice_maximum_fusion
  104.8 5.8 %collective-permute-done.1 = bf16[2,24,6,512]{3,2,1,0:T(8,128)(2,1)S(1)} collective-permute-done((bf16[2,24,6,512]{3,2,1,0:T(8,128)(2,1)S(1)}, bf16[2,24,6,512]{3,2,1,0:T(8,128)(2,1)S(1)}, u32[]{:S(2)}, u32[]{:S(2)}) %collective-permute-start.1) | collective-permute-done | bytes 294944 | tf_op jit(solution)/shard_map/ppermute | solution.py:20
  110.6 0.4 pad_maximum_fusion
  111.0 0.0 all-gather.4.cloned.1.call-done
  111.0 7.3 %convolution_convert_fusion = bf16[2304,1536]{1,0:T(8,128)(2,1)} fusion(bf16[2304,512]{1,0:T(8,128)(2,1)S(1)} %bitcast.91, bf16[512,1536]{0,1:T(8,128)(2,1)} %all-gather.4.cloned.1.call-done), kind=kOutput, calls=%fused_computation.29 | convolution fusion | flops 3627417600 | bytes 11010048 | tf_op jit(solution)/shard_map/dot_general | solution.py:86
  118.3 11.4 %reshape_reshape.6 = bf16[2,4,6,4,12,1536]{5,4,3,2,1,0:T(8,128)(2,1)} reshape(bf16[2304,1536]{1,0:T(8,128)(2,1)} %convolution_convert_fusion) | data formatting | bytes 14155776 | tf_op jit(solution)/shard_map/reshape;reshape | solution.py:37
  129.7 12.0 %copy.11 = bf16[4,4,2,6,12,1536]{5,1,0,4,3,2:T(4,128)(2,1)} copy(bf16[4,4,2,6,12,1536]{5,4,1,3,0,2:T(8,128)(2,1)} %bitcast.84) | data formatting | bytes 14155776 | tf_op jit(solution)/shard_map/transpose | solution.py:38
  141.6 32.5 %reshape.120 = bf16[16,144,3,16,32]{4,3,2,0,1:T(8,128)(2,1)} reshape(bf16[4,4,2,6,12,1536]{5,1,0,4,3,2:T(4,128)(2,1)} %copy.11) | data formatting | bytes 14155776 | tf_op jit(solution)/shard_map/reshape | solution.py:38
  174.1 24.0 %fusion.88 = (bf16[16,144,1,16,32]{4,3,2,0,1:T(8,128)(2,1)}, bf16[16,144,1,16,32]{4,3,2,0,1:T(8,128)(2,1)}, bf16[16,144,1,16,32]{4,3,2,0,1:T(8,128)(2,1)}) fusion(bf16[16,144,3,16,32]{4,3,2,0,1:T(8,128)(2,1)} %reshape.120), kind=kLoop, calls=%fused_computation.115 | loop fusion | bytes 14155776 | tf_op jit(solution)/shard_map/slice | solution.py:61
  198.1 12.3 %copy.21 = bf16[16,144,1,16,32]{1,4,3,0,2:T(8,128)(2,1)} copy(bf16[16,144,1,16,32]{4,3,2,0,1:T(8,128)(2,1)} %get-tuple-element.6) | data formatting | bytes 4718592
  210.4 12.4 %copy.22 = bf16[16,144,1,16,32]{1,4,3,0,2:T(8,128)(2,1)} copy(bf16[16,144,1,16,32]{4,3,2,0,1:T(8,128)(2,1)} %get-tuple-element.7) | data formatting | bytes 4718592
  222.8 12.3 %copy.20 = bf16[16,144,1,16,32]{1,4,3,0,2:T(8,128)(2,1)} copy(bf16[16,144,1,16,32]{4,3,2,0,1:T(8,128)(2,1)} %get-tuple-element.5) | data formatting | bytes 4718592
  235.1 19.9 %fusion.89 = (f32[16,16,144]{2,1,0:T(8,128)S(1)}, f32[16,16,144,144]{2,3,1,0:T(8,128)}) fusion(pred[16,144,144]{1,2,0:T(8,128)(4,1)S(1)} %compare_and_fusion, bf16[16,144,1,16,32]{1,4,3,0,2:T(8,128)(2,1)} %copy.22, bf16[16,144,1,16,32]{1,4,3,0,2:T(8,128)(2,1)} %copy.21), kind=kOutput, calls=%fused_computation.116 | convolution fusion | flops 360972416 | bytes 26431488 | tf_op jit(solution)/shard_map/sub | solution.py:59
  255.0 16.4 %convert_bitcast_fusion = bf16[16,144,16,32]{1,3,2,0:T(8,128)(2,1)} fusion(f32[16,16,144,144]{2,3,1,0:T(8,128)} %get-tuple-element.9, f32[16,16,144]{2,1,0:T(8,128)S(1)} %get-tuple-element.8, bf16[16,144,1,16,32]{1,4,3,0,2:T(8,128)(2,1)} %copy.20), kind=kOutput, calls=%fused_computation.58 | convolution fusion | flops 351535104 | bytes 26099712 | tf_op jit(solution)/shard_map/whqk,wkhd->wqhd/dot_general | solution.py:60
  271.4 11.5 %copy.17 = bf16[16,144,16,32]{3,2,0,1:T(8,128)(2,1)} copy(bf16[16,144,16,32]{1,3,2,0:T(8,128)(2,1)} %convert_bitcast_fusion) | data formatting | bytes 4718592 | tf_op jit(solution)/shard_map/convert_element_type | solution.py:63
  282.9 13.0 %reshape.121 = bf16[4,4,2,6,12,512]{5,1,0,4,3,2:T(4,128)(2,1)} reshape(bf16[16,144,16,32]{3,2,0,1:T(8,128)(2,1)} %copy.17) | data formatting | bytes 4718592 | tf_op jit(solution)/shard_map/reshape | solution.py:63
  295.9 3.9 copy.18
  299.8 2.1 reshape_reshape.7
  301.9 3.2 convolution_convert_fusion.1
  305.0 0.0 copy-start.4
  305.1 0.0 copy-start.1
  305.1 0.1 slice.71
  305.2 0.1 collective-permute-start.4
  305.3 7.7 %collective-permute-done.4 = bf16[2,24,6,512]{3,2,1,0:T(8,128)(2,1)S(1)} collective-permute-done((bf16[2,24,6,512]{3,2,1,0:T(8,128)(2,1)S(1)}, bf16[2,24,6,512]{3,2,1,0:T(8,128)(2,1)S(1)}, u32[]{:S(2)}, u32[]{:S(2)}) %collective-permute-start.4) | collective-permute-done | bytes 294944 | tf_op jit(solution)/shard_map/ppermute | solution.py:20
  313.0 0.1 pad_maximum_fusion.3
  313.1 0.1 collective-permute-start.5
  313.2 0.0 all-gather.8.cloned.1.call-update
  313.2 2.8 pad_maximum_fusion.1
  316.0 7.3 %collective-permute-done.5 = bf16[2,3,48,512]{3,2,1,0:T(8,128)(2,1)S(1)} collective-permute-done((bf16[2,3,48,512]{3,2,1,0:T(8,128)(2,1)S(1)}, bf16[2,3,48,512]{3,2,1,0:T(8,128)(2,1)S(1)}, u32[]{:S(2)}, u32[]{:S(2)}) %collective-permute-start.5) | collective-permute-done | bytes 294944 | tf_op jit(solution)/shard_map/ppermute | solution.py:20
  323.3 0.7 convert_reduce_fusion
  324.0 0.1 div.27
  324.0 2.7 fusion.23
  326.7 0.1 rsqrt.21
  326.8 1.9 maximum_convert_fusion
  328.7 0.0 copy-start.9
  328.7 2.2 fusion.24
  331.0 47.1 %fusion.110 = bf16[2304,2048]{1,0:T(8,128)(2,1)} fusion(bf16[512,2048]{0,1:T(8,128)(2,1)} %all-gather.6.cloned.1.call-done, bf16[2304,512]{1,0:T(8,128)(2,1)} %fusion.24, f32[512]{0:T(512)S(1)} %copy-done.9, f32[2304]{0:T(1024)S(1)} %rsqrt.21, f32[2304]{0:T(1024)S(1)} %div.27), kind=kOutput, calls=%fused_computation.8.clone.clone.1 | convolution fusion | flops 5144444928 | bytes 13914112 | tf_op jit(solution)/shard_map/dot_general | solution.py:111
  378.0 8.5 %fusion.18 = f32[2304,512]{1,0:T(8,128)S(1)} fusion(bf16[2048,512]{0,1:T(8,128)(2,1)} %all-gather.8.cloned.1.call-done, bf16[2304,2048]{1,0:T(8,128)(2,1)} %fusion.110), kind=kOutput, calls=%fused_computation.30 | convolution fusion | flops 4831838208 | bytes 16252928 | tf_op jit(solution)/shard_map/dot_general | solution.py:117
  386.5 2.5 add_convert_fusion
  (31 shorter events, 0.2 us)
Async XLA Ops:
  6.5 5.6 %copy-start = (bf16[1,2,24,48,512]{4,3,2,1,0:T(8,128)(2,1)S(1)}, bf16[1,2,24,48,512]{4,3,2,1,0:T(8,128)(2,1)}, u32[]{:S(2)}) copy-start(bf16[1,2,24,48,512]{4,3,2,1,0:T(8,128)(2,1)} %param.8) | copy-start | bytes 7077892
  6.5 5.6 %copy-start.8 = (f32[512]{0:T(512)S(1)}, f32[512]{0:T(512)}, u32[]{:S(2)}) copy-start(f32[512]{0:T(512)} %param.10) | copy-start | bytes 6148
  6.5 104.4 %all-gather.4.cloned.1.call-start = ((), (), s32[]{:S(2)}) async-start(), calls=%async_computation | async-start | bytes 1622016 | tf_op jit(solution)/shard_map/all_gather | solution.py:88
  7.3 12.4 %copy-start.7 = (s32[24,48]{1,0:T(8,128)S(1)}, s32[24,48]{1,0:T(8,128)}, u32[]{:S(2)}) copy-start(s32[24,48]{1,0:T(8,128)} %param.9) | copy-start | bytes 13828
  7.3 13.0 %copy-start.6 = (bf16[512,16]{0,1:T(8,128)(2,1)S(1)}, bf16[512,16]{0,1:T(8,128)(2,1)}, u32[]{:S(2)}) copy-start(bf16[512,16]{0,1:T(8,128)(2,1)} %param.12) | copy-start | bytes 49156
  7.3 323.7 %all-gather.6.cloned.1.call-start = ((), (), s32[]{:S(2)}) async-start(), calls=%async_computation.1 | async-start | bytes 2162688 | tf_op jit(solution)/shard_map/all_gather | solution.py:113
  13.1 1.4 copy-start.5
  14.5 88.2 %collective-permute-start = (bf16[2,3,48,512]{3,2,1,0:T(8,128)(2,1)S(1)}, bf16[2,3,48,512]{3,2,1,0:T(8,128)(2,1)S(1)}, u32[]{:S(2)}, u32[]{:S(2)}) collective-permute-start(bf16[2,3,48,512]{3,2,1,0:T(8,128)(2,1)S(1)} %slice.61), channel_id=1, source_target_pairs={{2,0},{4,2},{6,4},{0,6},{3,1},{5,3},{7,5},{1,7},{10,8},{12,10},{14... | collective-permute-start | bytes 884744 | tf_op jit(solution)/shard_map/ppermute | solution.py:20
  19.7 78.8 %collective-permute-start.2 = (bf16[3,48]{1,0:T(4,128)(2,1)S(1)}, bf16[3,48]{1,0:T(4,128)(2,1)S(1)}, u32[]{:S(2)}, u32[]{:S(2)}) collective-permute-start(bf16[3,48]{1,0:T(4,128)(2,1)S(1)} %slice.66), channel_id=1, source_target_pairs={{2,0},{4,2},{6,4},{0,6},{3,1},{5,3},{7,5},{1,7},{10,8},{12,10},{14... | collective-permute-start | bytes 872 | tf_op jit(solution)/shard_map/ppermute | solution.py:20
  20.2 357.8 %all-gather.8.cloned.1.call-start = ((), (), s32[]{:S(2)}) async-start(), calls=%async_computation.2 | async-start | bytes 2162688 | tf_op jit(solution)/shard_map/all_gather | solution.py:119
  98.5 3.9 collective-permute-start.3
  102.8 7.8 %collective-permute-start.1 = (bf16[2,24,6,512]{3,2,1,0:T(8,128)(2,1)S(1)}, bf16[2,24,6,512]{3,2,1,0:T(8,128)(2,1)S(1)}, u32[]{:S(2)}, u32[]{:S(2)}) collective-permute-start(bf16[2,24,6,512]{3,2,1,0:T(8,128)(2,1)S(1)} %pad_maximum_fusion.2), channel_id=1, source_target_pairs={{1,0},{0,1},{3,2},{2,3},{5,4},{4,5},{7,6},{6,7},{9,8},{8,9},{11,10... | collective-permute-start | bytes 884744 | tf_op jit(solution)/shard_map/ppermute | solution.py:20
  305.0 8.0 %copy-start.4 = (bf16[2304,512]{1,0:T(8,128)(2,1)}, bf16[2304,512]{1,0:T(8,128)(2,1)S(1)}, u32[]{:S(2)}) copy-start(bf16[2304,512]{1,0:T(8,128)(2,1)S(1)} %convolution_convert_fusion.1) | copy-start | bytes 7077892
  305.1 18.2 %copy-start.1 = (bf16[1,2,24,48,512]{4,3,2,1,0:T(8,128)(2,1)S(1)}, bf16[1,2,24,48,512]{4,3,2,1,0:T(8,128)(2,1)}, u32[]{:S(2)}) copy-start(bf16[1,2,24,48,512]{4,3,2,1,0:T(8,128)(2,1)} %param.8) | copy-start | bytes 7077892
  305.2 7.8 %collective-permute-start.4 = (bf16[2,24,6,512]{3,2,1,0:T(8,128)(2,1)S(1)}, bf16[2,24,6,512]{3,2,1,0:T(8,128)(2,1)S(1)}, u32[]{:S(2)}, u32[]{:S(2)}) collective-permute-start(bf16[2,24,6,512]{3,2,1,0:T(8,128)(2,1)S(1)} %slice.71), channel_id=1, source_target_pairs={{1,0},{0,1},{3,2},{2,3},{5,4},{4,5},{7,6},{6,7},{9,8},{8,9},{11,10... | collective-permute-start | bytes 884744 | tf_op jit(solution)/shard_map/ppermute | solution.py:20
  313.1 10.2 %collective-permute-start.5 = (bf16[2,3,48,512]{3,2,1,0:T(8,128)(2,1)S(1)}, bf16[2,3,48,512]{3,2,1,0:T(8,128)(2,1)S(1)}, u32[]{:S(2)}, u32[]{:S(2)}) collective-permute-start(bf16[2,3,48,512]{3,2,1,0:T(8,128)(2,1)S(1)} %pad_maximum_fusion.3), channel_id=1, source_target_pairs={{6,0},{0,2},{2,4},{4,6},{7,1},{1,3},{3,5},{5,7},{14,8},{8,10},{10,... | collective-permute-start | bytes 884744 | tf_op jit(solution)/shard_map/ppermute | solution.py:20
  316.0 7.3 %copy-start.2 = (bf16[2,21,48,512]{3,2,1,0:T(8,128)(2,1)}, bf16[2,21,48,512]{3,2,1,0:T(8,128)(2,1)S(1)}, u32[]{:S(2)}) copy-start(bf16[2,21,48,512]{3,2,1,0:T(8,128)(2,1)S(1)} %pad_maximum_fusion.1) | copy-start | bytes 6193156
  328.7 2.3 copy-start.9
  378.0 8.5 %copy-start.3 = (bf16[2,21,48,512]{3,2,1,0:T(8,128)(2,1)S(1)}, bf16[2,21,48,512]{3,2,1,0:T(8,128)(2,1)}, u32[]{:S(2)}) copy-start(bf16[2,21,48,512]{3,2,1,0:T(8,128)(2,1)} %copy-done.2) | copy-start | bytes 6193156
Sparse Core Ops, SparseCore 0:
  10.3 60.3 all-gather.3
  73.7 56.7 all-gather.5
  313.3 57.8 all-gather.7
where the time goes:
time: 402 us; the launch traced here: 396 us
  local copies, waits for them, and re-layouts  151 us (38%)
  matrix products  102 us (25%)
  blocking collectives  76.2 us (19%)
  waiting for transfers between devices  25.3 us (6%)
  other arithmetic  21.1 us (5%)
  between operations  13.7 us (3%)
  starting transfers between devices  6.03 us (2%)
    all_gather x1, blocking collectives, body(): lax.all_gather(w_proj, ('mem', 'lat', 'lon'), axis=1, tiled=True)  76.2 us
    dot_general x1, matrix products, body(): jnp.dot(normed2, lax.all_gather(w_up, ('mem', 'lat', 'lon'), axis=1, tile...  47.1 us
    unnamed x23, local copies, waits for them, and re-layouts  38.4 us
    reshape x1, local copies, waits for them, and re-layouts, attend(): windowed.transpose(1, 3, 0, 2, 4, 5)  32.5 us
    ppermute x6, waiting for transfers between devices, shifted_2(): return lax.ppermute(block, axis, route)  24.5 us
    slice x1, local copies, waits for them, and re-layouts, attend(): windowed[:, :, 2]  24 us
    sub x1, matrix products, attend(): attn_probs = jax.nn.softmax(scores, axis=-1).astype(jnp.bfloat16)  19.9 us
    dot_general x1, matrix products, attend(): jnp.einsum('whqk,wkhd->wqhd', attn_probs, windowed[:, :, 2], preferred_el...  16.4 us
  transfers between devices with their start and end apart: 9, of which 4 were waited for; matrix products, arithmetic and copies ran while one was open for 66% of the time, Pallas kernels for 0%

commit v1 on v0

v1 whole, which is shorter than its diff:
```python
import functools

import jax
import jax.numpy as jnp
from jax import lax
from jax.experimental import pallas as pl
from jax.experimental.pallas import tpu as pltpu
from jax.sharding import PartitionSpec as P

HDIM = 32
WLAT = 6
WLON = 12
SH = 3
SL = 6
LANES = 128
AXES = ("mem", "lat", "lon")
BIG = 1e9
EXP2_SCALE = 1.4426950408889634 / HDIM**0.5

eps = 1e-05

NT = (((1,), (1,)), ((), ()))
TN = (((0,), (0,)), ((), ()))


def dot32(a, b, dims):
    return lax.dot_general(a, b, dims, preferred_element_type=jnp.float32)


def shifted_2(block, axis, distance):
    devices = range(lax.axis_size(axis))
    route = [((i - distance) % len(devices), i) for i in devices]
    return lax.ppermute(block, axis, route)


def norm(values, gain):
    average = jnp.mean(values, axis=-1, keepdims=True)
    centred = values - average
    variance = jnp.mean(centred * centred, axis=-1, keepdims=True)
    return (centred * lax.rsqrt(variance + eps) * gain).astype(jnp.bfloat16)


def pieces(levels, wins):
    for w in range(wins):
        for l in range(levels):
            for r in range(WLAT):
                yield l, r, w * WLON, ((w * levels + l) * WLAT + r) * WLON


def attention_kernel(x_ref, hot_ref, gain_ref, wqkv_ref, wproj_ref, out_ref, grid_s, tok_s, qkv_s, mix_s):
    levels, _, cols, width = x_ref.shape
    wins = cols // WLON
    ntok = levels * WLAT * WLON
    grid_s[...] = x_ref[...].astype(jnp.float32)
    for l, r, c, t in pieces(levels, wins):
        tok_s[pl.ds(t, WLON), :] = grid_s[l, r, pl.ds(c, WLON), :]
    normed = norm(tok_s[...], gain_ref[...])
    for part in range(3):
        at = pl.ds(part * width, width)
        qkv_s[:, at] = dot32(normed, wqkv_ref[at, :], NT).astype(jnp.bfloat16)
    per = LANES // HDIM
    lane_head = lax.broadcasted_iota(jnp.int32, (ntok, LANES), 1) // HDIM
    for w in range(wins):
        rows = pl.ds(w * ntok, ntok)
        hot = hot_ref[0, rows, :]
        barred = ((hot.astype(jnp.float32) - 1.0) * BIG).astype(jnp.bfloat16)
        for g in range(width // LANES):
            q = qkv_s[rows, pl.ds(g * LANES, LANES)]
            k = qkv_s[rows, pl.ds(width + g * LANES, LANES)]
            v = qkv_s[rows, pl.ds(2 * width + g * LANES, LANES)]
            queries = jnp.concatenate(
                [jnp.concatenate([jnp.where(lane_head == h, q, jnp.zeros_like(q)), hot], axis=1) for h in range(per)],
                axis=0,
            )
            keys = jnp.concatenate([k, barred], axis=1)
            scores = dot32(keys, queries, NT)
            top = jnp.max(scores, axis=0, keepdims=True)
            probs = jnp.exp2((scores - top) * EXP2_SCALE)
            total = jnp.sum(probs, axis=0, keepdims=True)
            mixed = dot32(v, probs.astype(jnp.bfloat16), TN) * (1.0 / total)
            heads = [mixed[h * HDIM : (h + 1) * HDIM, h * ntok : (h + 1) * ntok] for h in range(per)]
            mix_s[rows, pl.ds(g * LANES, LANES)] = jnp.concatenate(heads, axis=0).T.astype(jnp.bfloat16)
    attn_out = dot32(mix_s[...], wproj_ref[...], NT).astype(jnp.bfloat16).astype(jnp.float32)
    out_ref[0] = (tok_s[...] + attn_out).astype(jnp.bfloat16)


def mlp_kernel(resid_ref, gain_ref, wup_ref, wdown_ref, out_ref, grid_s, tok_s):
    levels, _, cols, width = out_ref.shape
    hidden_all = wup_ref.shape[0]
    resid = resid_ref[0].astype(jnp.float32)
    normed = norm(resid, gain_ref[...])
    tok_s[...] = resid
    step = min(width, hidden_all)
    for at in range(0, hidden_all, step):
        pre = dot32(normed, wup_ref[pl.ds(at, step), :], NT)
        hidden = (0.5 * pre * (1.0 + lax.erf(pre * 0.5**0.5))).astype(jnp.bfloat16)
        tok_s[...] += dot32(hidden, wdown_ref[:, pl.ds(at, step)], NT)
    for l, r, c, t in pieces(levels, cols // WLON):
        grid_s[l, r, pl.ds(c, WLON), :] = tok_s[pl.ds(t, WLON), :]
    out_ref[...] = grid_s[...].astype(jnp.bfloat16)


def whole(shape):
    return pl.BlockSpec(shape, lambda b: (0,) * len(shape))


def body(fields, region, gain_attn, w_qkv, w_proj, gain_mlp, w_up, w_down):
    member = fields[0]
    levels, clat, clon, width = member.shape
    bands, wins = clat // WLAT, clon // WLON
    ntok = levels * WLAT * WLON
    btok = wins * ntok

    wqkv_t = lax.all_gather(w_qkv.T, AXES, axis=0, tiled=True)
    wproj_t = lax.all_gather(w_proj.T, AXES, axis=0, tiled=True)
    wup_t = lax.all_gather(w_up.T, AXES, axis=0, tiled=True)
    wdown_t = lax.all_gather(w_down.T, AXES, axis=0, tiled=True)

    region_ids = region.astype(jnp.bfloat16)
    row_ids = jnp.arange(clat, dtype=jnp.int32)
    nlat_all = clat * lax.axis_size("lat")
    north_side = (lax.axis_index("lat") * clat + SH + row_ids) % nlat_all < SH
    arrived, arrived_ids = shifted_2((member[:, :SH], region_ids[:SH]), "lat", -1)
    lat_band = jnp.concatenate([member[:, SH:], arrived], axis=1)
    band_ids = jnp.concatenate([region_ids[SH:], arrived_ids], axis=0)
    strip, strip_ids = shifted_2((lat_band[:, :, :SL], band_ids[:, :SL]), "lon", -1)
    shifted = jnp.concatenate([lat_band[:, :, SL:], strip], axis=2)
    shifted_ids = jnp.concatenate([band_ids[:, SL:], strip_ids], axis=1)

    groups = shifted_ids.astype(jnp.int32) + 3 * north_side[:, None].astype(jnp.int32)
    groups = groups.reshape(bands, 1, WLAT, wins, WLON).transpose(0, 3, 1, 2, 4)
    groups = jnp.broadcast_to(groups, (bands, wins, levels, WLAT, WLON)).reshape(bands, btok)
    hot = (groups[:, :, None] == jnp.arange(LANES, dtype=jnp.int32)).astype(jnp.bfloat16)

    grid_block = pl.BlockSpec((levels, WLAT, clon, width), lambda b: (0, b, 0, 0))
    tok_block = pl.BlockSpec((1, btok, width), lambda b: (b, 0, 0))
    f32_scratch = [pltpu.VMEM((levels, WLAT, clon, width), jnp.float32), pltpu.VMEM((btok, width), jnp.float32)]
    count = levels * clat * clon
    params = pltpu.CompilerParams(dimension_semantics=("arbitrary",), vmem_limit_bytes=56 * 2**20)
    resid = pl.pallas_call(
        attention_kernel,
        grid=(bands,),
        in_specs=[
            grid_block,
            pl.BlockSpec((1, btok, LANES), lambda b: (b, 0, 0)),
            whole((1, width)),
            whole(wqkv_t.shape),
            whole(wproj_t.shape),
        ],
        out_specs=tok_block,
        out_shape=jax.ShapeDtypeStruct((bands, btok, width), jnp.bfloat16),
        scratch_shapes=f32_scratch
        + [pltpu.VMEM((btok, 3 * width), jnp.bfloat16), pltpu.VMEM((btok, width), jnp.bfloat16)],
        compiler_params=params,
        cost_estimate=pl.CostEstimate(
            flops=24 * count * width * width // 3, bytes_accessed=4 * count * width, transcendentals=count * 4096
        ),
    )(shifted, hot, gain_attn[None], wqkv_t, wproj_t)
    out = pl.pallas_call(
        mlp_kernel,
        grid=(bands,),
        in_specs=[tok_block, whole((1, width)), whole(wup_t.shape), whole(wdown_t.shape)],
        out_specs=grid_block,
        out_shape=jax.ShapeDtypeStruct(member.shape, jnp.bfloat16),
        scratch_shapes=f32_scratch,
        compiler_params=params,
        cost_estimate=pl.CostEstimate(
            flops=4 * count * width * wup_t.shape[0], bytes_accessed=4 * count * width, transcendentals=count * 2048
        ),
    )(resid, gain_mlp[None], wup_t, wdown_t)

    arrived_cols = shifted_2(out[:, :, clon - SL :], "lon", 1)
    out = jnp.concatenate([arrived_cols, out[:, :, : clon - SL]], axis=2)
    arrived_rows = shifted_2(out[:, clat - SH :], "lat", 1)
    out = jnp.concatenate([arrived_rows, out[:, : clat - SH]], axis=1)
    return out[None]


def solution(mesh):
    columns = P(None, AXES)
    in_specs = (P("mem", None, "lat", "lon", None), P("lat", "lon"), P(), columns, columns, P(), columns, columns)
    out_specs = P("mem", None, "lat", "lon", None)
    return jax.shard_map(body, mesh=mesh, in_specs=in_specs, out_specs=out_specs, check_vma=False)
```

time: 402 us -> 236 us (0.59); the launches traced: 396 us -> 236 us
  local copies, waits for them, and re-layouts: 151 us -> 4.18 us
  matrix products: 102 us -> 0 us
  waiting for transfers between devices: 25.3 us -> 80 us
  Pallas kernels: 0 us -> 46.9 us
  other arithmetic: 21.1 us -> 8.1 us
    dot_general x5 -> x0, matrix products: 82.4 us -> none  [the longest x1 47.1 us: body(): jnp.dot(normed2, lax.all_gather(w_up, ('mem', 'lat', 'lon'), axis=1, tile...]
    all_gather x3, waiting for transfers between devices: 0.02 us -> 49.1 us  [the longest x1 49.1 us: body(): wdown_t = lax.all_gather(w_down.T, AXES, axis=0, tiled=True)]
    pallas_call x0 -> x2, Pallas kernels: none -> 46.9 us  [the longest x1 31.3 us: body(): pl.pallas_call(attention_kernel, grid=(bands,), in_specs=[grid_block, pl....]
    reshape x2 -> x0, local copies, waits for them, and re-layouts: 45.4 us -> none  [the longest x1 32.5 us: attend(): windowed.transpose(1, 3, 0, 2, 4, 5)]
    unnamed x23 -> x2, local copies, waits for them, and re-layouts: 38.4 us -> 0.01 us
    slice x4 -> x3, local copies, waits for them, and re-layouts: 25.9 us -> 3.94 us  [the longest x1 1.72 us: body(): lat_band = jnp.concatenate([member[:, SH:], arrived], axis=1)]
    sub x1 -> x0, matrix products: 19.9 us -> none  [attend(): attn_probs = jax.nn.softmax(scores, axis=-1).astype(jnp.bfloat16)]
    transpose x4 -> x0, local copies, waits for them, and re-layouts: 16 us -> none  [the longest x1 12 us: attend(): windowed.transpose(1, 3, 0, 2, 4, 5)]
  transfers between devices with their start and end apart: 9 -> 9, of which waited for: 4 -> 5; matrix products, arithmetic and copies ran while one was open for 66% -> 3% of each run, Pallas kernels for 0% -> 13%
where the time goes in v1:
time: 236 us
  waiting for transfers between devices  80 us (34%)
  blocking collectives  75.3 us (32%)
  Pallas kernels  46.9 us (20%)
  between operations  13.2 us (6%)
  other arithmetic  8.1 us (3%)
  starting transfers between devices  7.86 us (3%)
  local copies, waits for them, and re-layouts  4.18 us (2%)
    all_gather x1, blocking collectives, body(): wproj_t = lax.all_gather(w_proj.T, AXES, axis=0, tiled=True)  75.3 us
    all_gather x1, waiting for transfers between devices, body(): wdown_t = lax.all_gather(w_down.T, AXES, axis=0, tiled=True)  49.1 us
    pallas_call x1, Pallas kernels, body(): pl.pallas_call(attention_kernel, grid=(bands,), in_specs=[grid_block, pl....  31.3 us
    ppermute x6, waiting for transfers between devices, shifted_2(): return lax.ppermute(block, axis, route)  28.9 us
    pallas_call x1, Pallas kernels, body(): pl.pallas_call(mlp_kernel, grid=(bands,), in_specs=[tok_block, whole((1,...  15.6 us
    ppermute x6, starting transfers between devices, shifted_2(): return lax.ppermute(block, axis, route)  7.79 us
  transfers between devices with their start and end apart: 9, of which 5 were waited for; matrix products, arithmetic and copies ran while one was open for 3% of the time, Pallas kernels for 13%

profile of v1, /device:TPU:0, one launch (start us, length us, event | category | flops | bytes accessed | tf_op | source)
XLA Modules:
  0.0 235.6 jit_solution(5094613412657364581)
XLA Ops:
  6.5 0.0 all-gather.4.cloned.1.call-start
  6.5 0.7 all-gather.4.cloned.1.call-update
  7.3 0.0 all-gather.6.cloned.1.call-start
  7.3 0.7 all-gather.6.cloned.1.call-update
  8.0 0.0 all-gather.8.cloned.1.call-start
  8.1 0.7 all-gather.8.cloned.1.call-update
  8.7 1.0 slice.49
  9.7 5.1 %collective-permute-start = (bf16[2,3,48,512]{3,2,1,0:T(8,128)(2,1)S(1)}, bf16[2,3,48,512]{3,2,1,0:T(8,128)(2,1)S(1)}, u32[]{:S(2)}, u32[]{:S(2)}) collective-permute-start(bf16[2,3,48,512]{3,2,1,0:T(8,128)(2,1)S(1)} %slice.49), channel_id=1, source_target_pairs={{2,0},{4,2},{6,4},{0,6},{3,1},{5,3},{7,5},{1,7},{10,8},{12,10},{14... | collective-permute-start | bytes 884744 | tf_op jit(solution)/shard_map/ppermute | solution.py:33
  14.9 0.7 convert_element_type.20
  15.6 0.4 collective-permute-start.2
  16.0 75.3 %all_gather.13.wproj_ref = bf16[512,512]{1,0:T(8,128)(2,1)} all-gather(bf16[16,512]{1,0:T(8,128)(2,1)} %bitcast.21), channel_id=1, replica_groups=mesh['mem'=4,'lat'=4,'lon'=2] {'mem','lat','lon'}, dimensions={0}, use_global_device_ids=true | all-gather | bytes 540672 | tf_op jit(solution)/shard_map/all_gather | solution.py:115
  91.3 1.7 slice.48
  93.0 0.0 collective-permute-done.2
  93.1 0.1 collective-permute-start.3
  93.1 0.1 slice_maximum_fusion.1
  93.2 3.5 %collective-permute-done.3 = bf16[24,6]{1,0:T(8,128)(2,1)S(1)} collective-permute-done((bf16[24,6]{1,0:T(8,128)(2,1)S(1)}, bf16[24,6]{1,0:T(8,128)(2,1)S(1)}, u32[]{:S(2)}, u32[]{:S(2)}) %collective-permute-start.3) | collective-permute-done | bytes 320 | tf_op jit(solution)/shard_map/ppermute | solution.py:33
  96.8 0.1 maximum_convert_fusion
  96.8 0.1 reshape.37
  96.9 0.1 add_bitcast_fusion
  97.1 0.1 eq.17
  97.2 0.0 collective-permute-done
  97.2 0.1 collective-permute-start.1
  97.3 1.2 fusion.2.hot_ref
  98.5 0.6 slice_maximum_fusion
  99.1 5.9 %collective-permute-done.1 = bf16[2,24,6,512]{3,2,1,0:T(8,128)(2,1)S(1)} collective-permute-done((bf16[2,24,6,512]{3,2,1,0:T(8,128)(2,1)S(1)}, bf16[2,24,6,512]{3,2,1,0:T(8,128)(2,1)S(1)}, u32[]{:S(2)}, u32[]{:S(2)}) %collective-permute-start.1) | collective-permute-done | bytes 294944 | tf_op jit(solution)/shard_map/ppermute | solution.py:33
  105.1 1.8 pad_maximum_fusion.1.x_ref
  106.8 0.0 all-gather.4.cloned.1.call-done.wqkv_ref
  106.8 31.3 %shard_map.82.resid_ref = bf16[4,576,512]{2,1,0:T(8,128)(2,1)} custom-call(bf16[2,24,48,512]{3,2,1,0:T(8,128)(2,1)} %pad_maximum_fusion.1.x_ref, bf16[4,576,128]{2,1,0:T(8,128)(2,1)} %fusion.2.hot_ref, f32[1,512]{1,0:T(1,128)} %bitcast.22, bf16[1536,512]{1,0:T(8,128)(2,1)} %all-gather.4.cloned.1.call-done.wqkv_ref, bf16[512,512]{1,0:T(8,128)(2,1)} %all_gather.13.wproj_ref), custom_call_target="tpu_custom_call" | custom-call | flops 4831838208 | bytes 4718592 | tf_op jit(solution)/shard_map/pallas_call | solution.py:140
  138.2 0.0 all-gather.6.cloned.1.call-done.wup_ref
  138.2 49.1 %all-gather.8.cloned.1.call-done.wdown_ref = bf16[512,2048]{1,0:T(8,128)(2,1)} async-done(((bf16[16,2048]{1,0:T(8,128)(2,1)}), bf16[512,2048]{1,0:T(8,128)(2,1)}) %all-gather.8.cloned.1.call-update) | async-done | bytes 2097168 | tf_op jit(solution)/shard_map/all_gather | solution.py:117
  187.2 15.6 %shard_map.83 = bf16[2,24,48,512]{3,2,1,0:T(8,128)(2,1)} custom-call(bf16[4,576,512]{2,1,0:T(8,128)(2,1)} %shard_map.82.resid_ref, f32[1,512]{1,0:T(1,128)} %bitcast.23, bf16[2048,512]{1,0:T(8,128)(2,1)} %all-gather.6.cloned.1.call-done.wup_ref, bf16[512,2048]{1,0:T(8,128)(2,1)} %all-gather.8.cloned.1.call-done.wdown_ref), custom_call_target="tpu_custom_call" | custom-call | flops 9663676416 | bytes 4718592 | tf_op jit(solution)/shard_map/pallas_call | solution.py:159
  202.8 0.0 copy-start
  202.8 1.2 slice.56
  204.1 1.5 collective-permute-start.4
  205.6 9.8 %collective-permute-done.4 = bf16[2,24,6,512]{3,2,1,0:T(8,128)(2,1)S(1)} collective-permute-done((bf16[2,24,6,512]{3,2,1,0:T(8,128)(2,1)S(1)}, bf16[2,24,6,512]{3,2,1,0:T(8,128)(2,1)S(1)}, u32[]{:S(2)}, u32[]{:S(2)}) %collective-permute-start.4) | collective-permute-done | bytes 294944 | tf_op jit(solution)/shard_map/ppermute | solution.py:33
  215.4 1.0 pad_maximum_fusion.3
  216.4 0.6 collective-permute-start.5
  217.0 9.6 %collective-permute-done.5 = bf16[2,3,48,512]{3,2,1,0:T(8,128)(2,1)S(1)} collective-permute-done((bf16[2,3,48,512]{3,2,1,0:T(8,128)(2,1)S(1)}, bf16[2,3,48,512]{3,2,1,0:T(8,128)(2,1)S(1)}, u32[]{:S(2)}, u32[]{:S(2)}) %collective-permute-start.5) | collective-permute-done | bytes 294944 | tf_op jit(solution)/shard_map/ppermute | solution.py:33
  226.6 0.0 copy-done
  226.6 2.5 %fusion.1 = bf16[1,2,24,48,512]{4,3,2,1,0:T(8,128)(2,1)} fusion(bf16[2,24,42,512]{3,2,1,0:T(8,128)(2,1)S(1)} %bitcast.15, bf16[2,24,6,512]{3,2,1,0:T(8,128)(2,1)S(1)} %collective-permute-done.4, bf16[2,3,48,512]{3,2,1,0:T(8,128)(2,1)S(1)} %collective-permute-done.5), kind=kLoop, calls=%fused_computation.2 | loop fusion | flops 7077888 | bytes 5013504 | tf_op jit(solution)/shard_map/broadcast_in_dim | solution.py:176
  (7 shorter events, 0.1 us)
Async XLA Ops:
  6.5 100.3 %all-gather.4.cloned.1.call-start = ((), (), s32[]{:S(2)}) async-start(), calls=%async_computation | async-start | bytes 1622016 | tf_op jit(solution)/shard_map/all_gather | solution.py:114
  7.3 130.9 %all-gather.6.cloned.1.call-start = ((), (), s32[]{:S(2)}) async-start(), calls=%async_computation.1 | async-start | bytes 2162688 | tf_op jit(solution)/shard_map/all_gather | solution.py:116
  8.0 179.2 %all-gather.8.cloned.1.call-start = ((), (), s32[]{:S(2)}) async-start(), calls=%async_computation.2 | async-start | bytes 2162688 | tf_op jit(solution)/shard_map/all_gather | solution.py:117
  9.7 87.5 %collective-permute-start = (bf16[2,3,48,512]{3,2,1,0:T(8,128)(2,1)S(1)}, bf16[2,3,48,512]{3,2,1,0:T(8,128)(2,1)S(1)}, u32[]{:S(2)}, u32[]{:S(2)}) collective-permute-start(bf16[2,3,48,512]{3,2,1,0:T(8,128)(2,1)S(1)} %slice.49), channel_id=1, source_target_pairs={{2,0},{4,2},{6,4},{0,6},{3,1},{5,3},{7,5},{1,7},{10,8},{12,10},{14... | collective-permute-start | bytes 884744 | tf_op jit(solution)/shard_map/ppermute | solution.py:33
  15.6 77.5 %collective-permute-start.2 = (bf16[3,48]{1,0:T(4,128)(2,1)S(1)}, bf16[3,48]{1,0:T(4,128)(2,1)S(1)}, u32[]{:S(2)}, u32[]{:S(2)}) collective-permute-start(bf16[3,48]{1,0:T(4,128)(2,1)S(1)} %slice.53), channel_id=1, source_target_pairs={{2,0},{4,2},{6,4},{0,6},{3,1},{5,3},{7,5},{1,7},{10,8},{12,10},{14... | collective-permute-start | bytes 872 | tf_op jit(solution)/shard_map/ppermute | solution.py:33
  93.1 3.7 %collective-permute-start.3 = (bf16[24,6]{1,0:T(8,128)(2,1)S(1)}, bf16[24,6]{1,0:T(8,128)(2,1)S(1)}, u32[]{:S(2)}, u32[]{:S(2)}) collective-permute-start(bf16[24,6]{1,0:T(8,128)(2,1)S(1)} %pad_maximum_fusion.4), channel_id=1, source_target_pairs={{1,0},{0,1},{3,2},{2,3},{5,4},{4,5},{7,6},{6,7},{9,8},{8,9},{11,10... | collective-permute-start | bytes 872 | tf_op jit(solution)/shard_map/ppermute | solution.py:33
  97.2 7.8 %collective-permute-start.1 = (bf16[2,24,6,512]{3,2,1,0:T(8,128)(2,1)S(1)}, bf16[2,24,6,512]{3,2,1,0:T(8,128)(2,1)S(1)}, u32[]{:S(2)}, u32[]{:S(2)}) collective-permute-start(bf16[2,24,6,512]{3,2,1,0:T(8,128)(2,1)S(1)} %pad_maximum_fusion.2), channel_id=1, source_target_pairs={{1,0},{0,1},{3,2},{2,3},{5,4},{4,5},{7,6},{6,7},{9,8},{8,9},{11,10... | collective-permute-start | bytes 884744 | tf_op jit(solution)/shard_map/ppermute | solution.py:33
  202.8 23.7 %copy-start = (bf16[2,24,48,512]{3,2,1,0:T(8,128)(2,1)S(1)}, bf16[2,24,48,512]{3,2,1,0:T(8,128)(2,1)}, u32[]{:S(2)}) copy-start(bf16[2,24,48,512]{3,2,1,0:T(8,128)(2,1)} %shard_map.83) | copy-start | bytes 7077892
  204.1 11.3 %collective-permute-start.4 = (bf16[2,24,6,512]{3,2,1,0:T(8,128)(2,1)S(1)}, bf16[2,24,6,512]{3,2,1,0:T(8,128)(2,1)S(1)}, u32[]{:S(2)}, u32[]{:S(2)}) collective-permute-start(bf16[2,24,6,512]{3,2,1,0:T(8,128)(2,1)S(1)} %slice.56), channel_id=1, source_target_pairs={{1,0},{0,1},{3,2},{2,3},{5,4},{4,5},{7,6},{6,7},{9,8},{8,9},{11,10... | collective-permute-start | bytes 884744 | tf_op jit(solution)/shard_map/ppermute | solution.py:33
  216.4 10.1 %collective-permute-start.5 = (bf16[2,3,48,512]{3,2,1,0:T(8,128)(2,1)S(1)}, bf16[2,3,48,512]{3,2,1,0:T(8,128)(2,1)S(1)}, u32[]{:S(2)}, u32[]{:S(2)}) collective-permute-start(bf16[2,3,48,512]{3,2,1,0:T(8,128)(2,1)S(1)} %pad_maximum_fusion.3), channel_id=1, source_target_pairs={{6,0},{0,2},{2,4},{4,6},{7,1},{1,3},{3,5},{5,7},{14,8},{8,10},{10,... | collective-permute-start | bytes 884744 | tf_op jit(solution)/shard_map/ppermute | solution.py:33
Sparse Core Ops, SparseCore 0:
  10.3 58.7 all-gather.3
  72.1 56.8 all-gather.5
  132.0 55.2 all-gather.7
